TPU v7x, 16 devices: a whole 2x2x2 slice. The times are simulated.
16 devices in a mesh: dp: 2 (over z), col: 2 (over y), fsdp: 4 (over x, core).
Axes of the slice: x: 2, y: 2, z: 2, core: 2. Of those that a mesh axis runs over, the one named last changes fastest.
Arguments:
- x_act: bfloat16 [65536, 768], P(('dp', 'col', 'fsdp'))
- dy_out: bfloat16 [65536, 768], P(('dp', 'col', 'fsdp'))
- w_gate: bfloat16 [768, 2048], P(None, ('col', 'fsdp'))
- w_up: bfloat16 [768, 2048], P(None, ('col', 'fsdp'))
- w_down: bfloat16 [2048, 768], P(('col', 'fsdp'))
- v_gate: bfloat16 [768, 2048], P(None, ('col', 'fsdp'))
- v_up: bfloat16 [768, 2048], P(None, ('col', 'fsdp'))
- v_down: bfloat16 [2048, 768], P(('col', 'fsdp'))
- g_next: float32 [16, 3, 768, 2048], P(('dp', 'col', 'fsdp'))
Outputs:
- output 1: bfloat16 [65536, 768], P(('dp', 'col', 'fsdp'))
- output 2: float32 [3, 768, 2048], P(None, None, ('col', 'fsdp'))
- output 3: float32 [16, 3, 768, 2048], P(('dp', 'col', 'fsdp'))
- output 4: bfloat16 [768, 2048], replicated
- output 5: bfloat16 [768, 2048], replicated
- output 6: bfloat16 [2048, 768], replicated
All inputs are finite; a program needn't handle non-finite values.
Results may differ from a plain program's by a relative error of at most 0.0105826.
Values are sent between devices in bfloat16 or wider.
A program may use at most 1 GiB of HBM per device.

v0:
```python
import jax
import jax.numpy as jnp
from jax import lax
from jax.sharding import PartitionSpec as P

ALL_AXES = ('dp', 'col', 'fsdp')
FSDP_AXES = ('col', 'fsdp')


def local_backward(x_loc, dy_loc, gate_full, up_full, down_full):
    pre_gate = jnp.dot(x_loc, gate_full, preferred_element_type=jnp.float32)
    pre_up = jnp.dot(x_loc, up_full, preferred_element_type=jnp.float32)
    sig_gate = jax.nn.sigmoid(pre_gate)
    act_gate = pre_gate * sig_gate
    hidden = (act_gate * pre_up).astype(jnp.bfloat16)
    d_hidden = jnp.einsum('td,fd->tf', dy_loc, down_full, preferred_element_type=jnp.float32)
    d_gate = (d_hidden * pre_up * sig_gate * (1.0 + pre_gate * (1.0 - sig_gate))).astype(jnp.bfloat16)
    d_up = (d_hidden * act_gate).astype(jnp.bfloat16)
    dx_loc = (jnp.einsum('tf,df->td', d_gate, gate_full, preferred_element_type=jnp.float32)
              + jnp.einsum('tf,df->td', d_up, up_full, preferred_element_type=jnp.float32)).astype(jnp.bfloat16)
    grad_local = jnp.stack([
        jnp.einsum('td,tf->df', x_loc, d_gate, preferred_element_type=jnp.float32),
        jnp.einsum('td,tf->df', x_loc, d_up, preferred_element_type=jnp.float32),
        jnp.einsum('td,tf->df', dy_loc, hidden, preferred_element_type=jnp.float32),
    ])
    return dx_loc, grad_local


def solution(mesh):
    def device_step(x_loc, dy_loc, w_gate, w_up, w_down, v_gate, v_up, v_down, g_next):
        gate_full = lax.all_gather(w_gate, FSDP_AXES, axis=1, tiled=True)
        up_full = lax.all_gather(w_up, FSDP_AXES, axis=1, tiled=True)
        down_full = lax.all_gather(w_down, FSDP_AXES, axis=0, tiled=True)
        v_gate_full = lax.all_gather(v_gate, FSDP_AXES, axis=1, tiled=True)
        v_up_full = lax.all_gather(v_up, FSDP_AXES, axis=1, tiled=True)
        v_down_full = lax.all_gather(v_down, FSDP_AXES, axis=0, tiled=True)
        grad_shard = lax.psum_scatter(g_next[0].astype(jnp.bfloat16), FSDP_AXES, scatter_dimension=2, tiled=True)
        grad_next = lax.psum(grad_shard.astype(jnp.float32), 'dp')
        dx_loc, grad_local = local_backward(x_loc, dy_loc, gate_full, up_full, down_full)
        return dx_loc, grad_next, grad_local[None], v_gate_full, v_up_full, v_down_full

    row_spec = P(ALL_AXES, None)
    col_shard = P(None, FSDP_AXES)
    row_shard = P(FSDP_AXES, None)
    dev_spec = P(ALL_AXES, None, None, None)
    return jax.shard_map(
        device_step, mesh=mesh,
        in_specs=(row_spec, row_spec, col_shard, col_shard, row_shard, col_shard, col_shard, row_shard, dev_spec),
        out_specs=(row_spec, P(None, None, FSDP_AXES), dev_spec, P(), P(), P()),
        check_vma=False)
```

profile of v0, /device:TPU:0, one launch (start us, length us, event | category | flops | bytes accessed | tf_op | source)
XLA Modules:
  0.0 358.5 jit_solution(2438572119514652059)
XLA Ops:
  7.2 0.7 all-gather.11.cloned.1.call-update
  7.9 0.7 all-gather.9.cloned.1.call-update
  8.7 0.7 all-gather.7.cloned.1.call-update
  9.4 0.5 all-gather.13.cloned.1.call-update
  10.0 0.5 all-gather.15.cloned.1.call-update
  10.6 0.5 all-gather.17.cloned.1.call-update
  11.2 9.9 %convert_bitcast_fusion = bf16[3,768,2048]{2,1,0:T(8,128)(2,1)} fusion(f32[1,3,768,2048]{3,2,1,0:T(8,128)} %param.17), kind=kLoop, calls=%fused_computation.8 | loop fusion | flops 4718592 | bytes 28311552 | tf_op jit(solution)/shard_map/convert_element_type | solution.py:37
  21.1 20.3 %all-gather.11.cloned.1.call-done = bf16[768,2048]{1,0:T(8,128)(2,1)} async-done(((bf16[768,256]{1,0:T(8,128)(2,1)}), bf16[768,2048]{1,0:T(8,128)(2,1)}) %all-gather.11.cloned.1.call-update) | async-done | bytes 3145744 | tf_op jit(solution)/shard_map/all_gather | solution.py:31
  41.4 22.0 %fusion.6 = f32[4096,2048]{1,0:T(8,128)} fusion(bf16[4096,768]{1,0:T(8,128)(2,1)} %param.9, bf16[768,2048]{1,0:T(8,128)(2,1)} %all-gather.11.cloned.1.call-done), kind=kOutput, calls=%fused_computation.14 | convolution fusion | flops 12884901888 | bytes 42991616 | tf_op jit(solution)/shard_map/dot_general | solution.py:11
  63.4 8.6 %all-gather.9.cloned.1.call-done = bf16[768,2048]{1,0:T(8,128)(2,1)} async-done(((bf16[768,256]{1,0:T(8,128)(2,1)}), bf16[768,2048]{1,0:T(8,128)(2,1)}) %all-gather.9.cloned.1.call-update) | async-done | bytes 3145744 | tf_op jit(solution)/shard_map/all_gather | solution.py:32
  72.0 22.3 %fusion.5 = f32[4096,2048]{1,0:T(8,128)} fusion(bf16[4096,768]{1,0:T(8,128)(2,1)} %param.9, bf16[768,2048]{1,0:T(8,128)(2,1)} %all-gather.9.cloned.1.call-done), kind=kOutput, calls=%fused_computation.13 | convolution fusion | flops 12884901888 | bytes 42991616 | tf_op jit(solution)/shard_map/dot_general | solution.py:12
  94.3 7.8 %all-gather.7.cloned.1.call-done = bf16[2048,768]{1,0:T(8,128)(2,1)} async-done(((bf16[256,768]{1,0:T(8,128)(2,1)}), bf16[2048,768]{1,0:T(8,128)(2,1)}) %all-gather.7.cloned.1.call-update) | async-done | bytes 3145744 | tf_op jit(solution)/shard_map/all_gather | solution.py:33
  102.0 42.6 %multiply_convert_fusion.1 = (bf16[4096,2048]{1,0:T(8,128)(2,1)}, bf16[4096,2048]{1,0:T(8,128)(2,1)}) fusion(f32[4096,2048]{1,0:T(8,128)} %fusion.6, f32[4096,2048]{1,0:T(8,128)} %fusion.5, bf16[4096,768]{1,0:T(8,128)(2,1)} %param.10, bf16[2048,768]{1,0:T(8,128)(2,1)} %all-gather.7.cloned.1.call-done), kind=kOutput, calls=%fused_computation.1 | convolution fusion | flops 12993953792 | bytes 110100480 | tf_op jit(solution)/shard_map/td,fd->tf/dot_general | solution.py:16
  144.6 19.7 %convolution_bitcast_fusion = f32[1,768,2048]{1,2,0:T(8,128)S(1)} fusion(bf16[4096,2048]{1,0:T(8,128)(2,1)} %get-tuple-element.12, bf16[4096,768]{1,0:T(8,128)(2,1)} %param.9), kind=kOutput, calls=%fused_computation.9 | convolution fusion | flops 12884901888 | bytes 29360128 | tf_op jit(solution)/shard_map/td,tf->df/dot_general | solution.py:23
  164.4 19.2 %convolution_bitcast_fusion.1 = f32[1,768,2048]{1,2,0:T(8,128)} fusion(bf16[4096,2048]{1,0:T(8,128)(2,1)} %get-tuple-element.13, bf16[4096,768]{1,0:T(8,128)(2,1)S(1)} %copy-done.2), kind=kOutput, calls=%fused_computation.10 | convolution fusion | flops 12884901888 | bytes 29360128 | tf_op jit(solution)/shard_map/td,tf->df/dot_general | solution.py:22
  183.6 28.7 %fusion.3 = f32[1,768,2048]{1,2,0:T(8,128)} fusion(bf16[4096,768]{1,0:T(8,128)(2,1)} %param.10, f32[4096,2048]{1,0:T(8,128)} %fusion.5, f32[4096,2048]{1,0:T(8,128)} %fusion.6), kind=kOutput, calls=%fused_computation.11 | convolution fusion | flops 12935233536 | bytes 79691776 | tf_op jit(solution)/shard_map/td,tf->df/dot_general | solution.py:24
  212.4 12.1 %maximum_bitcast_fusion = f32[1,3,768,2048]{2,3,1,0:T(8,128)} fusion(f32[1,768,2048]{1,2,0:T(8,128)} %fusion.3, f32[1,768,2048]{1,2,0:T(8,128)S(1)} %convolution_bitcast_fusion, f32[1,768,2048]{1,2,0:T(8,128)} %convolution_bitcast_fusion.1), kind=kLoop, calls=%fused_computation.5 | loop fusion | flops 9437184 | bytes 37748736 | tf_op jit(solution)/shard_map/broadcast_in_dim | solution.py:40
  224.5 18.8 %copy.15 = f32[1,3,768,2048]{3,2,1,0:T(8,128)} copy(f32[1,3,768,2048]{2,3,1,0:T(8,128)} %maximum_bitcast_fusion) | data formatting | bytes 37748736
  243.3 18.4 %fusion.7 = f32[4096,768]{1,0:T(8,128)} fusion(bf16[4096,2048]{1,0:T(8,128)(2,1)} %get-tuple-element.13, bf16[768,2048]{1,0:T(8,128)(2,1)S(1)} %copy-done.3), kind=kOutput, calls=%fused_computation.15 | convolution fusion | flops 12884901888 | bytes 32505856 | tf_op jit(solution)/shard_map/tf,df->td/dot_general | solution.py:19
  261.6 21.8 %add_convert_fusion = bf16[4096,768]{1,0:T(8,128)(2,1)} fusion(f32[4096,768]{1,0:T(8,128)} %fusion.7, bf16[4096,2048]{1,0:T(8,128)(2,1)} %get-tuple-element.12, bf16[768,2048]{1,0:T(8,128)(2,1)} %all-gather.9.cloned.1.call-done), kind=kOutput, calls=%fused_computation.7 | convolution fusion | flops 12891193344 | bytes 38797312 | tf_op jit(solution)/shard_map/tf,df->td/dot_general | solution.py:20
  283.5 60.3 %all-reduce.1 = f32[3,768,256]{2,1,0:T(8,128)} all-reduce(bf16[3,768,256]{2,1,0:T(8,128)(2,1)} %reduce-scatter.2.cloned.1.call-done), channel_id=1, replica_groups=mesh['dp'=2,'col'=2,'fsdp'=4] {'dp'}, use_global_device_ids=true, to_apply=%region_1.0 | all-reduce | flops 589824 | bytes 3538944 | tf_op jit(solution)/shard_map/psum | solution.py:38
  343.7 1.7 copy.21
  345.4 4.4 %copy.22 = bf16[768,2048]{1,0:T(8,128)(2,1)} copy(bf16[768,2048]{1,0:T(8,128)(2,1)} %all-gather.15.cloned.1.call-done) | data formatting | bytes 6291456
  349.8 1.7 copy.23
  (20 shorter events, 0.3 us)
Async XLA Ops:
  7.2 34.2 %all-gather.11.cloned.1.call-start = ((), (), s32[]{:S(2)}) async-start(), calls=%async_computation.3 | async-start | bytes 3538944 | tf_op jit(solution)/shard_map/all_gather | solution.py:31
  7.9 64.1 %all-gather.9.cloned.1.call-start = ((), (), s32[]{:S(2)}) async-start(), calls=%async_computation.2 | async-start | bytes 3538944 | tf_op jit(solution)/shard_map/all_gather | solution.py:32
  8.6 93.4 %all-gather.7.cloned.1.call-start = ((), (), s32[]{:S(2)}) async-start(), calls=%async_computation.1 | async-start | bytes 3538944 | tf_op jit(solution)/shard_map/all_gather | solution.py:33
  9.4 233.9 %all-gather.13.cloned.1.call-start = ((), (), s32[]{:S(2)}) async-start(), calls=%async_computation.5 | async-start | bytes 3538944 | tf_op jit(solution)/shard_map/all_gather | solution.py:34
  10.0 233.3 %all-gather.15.cloned.1.call-start = ((), (), s32[]{:S(2)}) async-start(), calls=%async_computation.6 | async-start | bytes 3538944 | tf_op jit(solution)/shard_map/all_gather | solution.py:35
  10.5 232.7 %all-gather.17.cloned.1.call-start = ((), (), s32[]{:S(2)}) async-start(), calls=%async_computation.7 | async-start | bytes 3538944 | tf_op jit(solution)/shard_map/all_gather | solution.py:36
  11.1 272.3 %reduce-scatter.2.cloned.1.call-start = ((), (), s32[]{:S(2)}) async-start(), calls=%async_computation.4 | async-start | bytes 10616832 | tf_op jit(solution)/shard_map/reduce_scatter | solution.py:37
  144.6 19.8 %copy-start.2 = (bf16[4096,768]{1,0:T(8,128)(2,1)S(1)}, bf16[4096,768]{1,0:T(8,128)(2,1)}, u32[]{:S(2)}) copy-start(bf16[4096,768]{1,0:T(8,128)(2,1)} %param.9) | copy-start | bytes 18874372
  224.5 18.8 %copy-start.3 = (bf16[768,2048]{1,0:T(8,128)(2,1)S(1)}, bf16[768,2048]{1,0:T(8,128)(2,1)}, u32[]{:S(2)}) copy-start(bf16[768,2048]{1,0:T(8,128)(2,1)} %all-gather.11.cloned.1.call-done) | copy-start | bytes 9437188
  261.6 82.1 %copy-start = (bf16[768,2048]{1,0:T(8,128)(2,1)S(1)}, bf16[768,2048]{1,0:T(8,128)(2,1)}, u32[]{:S(2)}) copy-start(bf16[768,2048]{1,0:T(8,128)(2,1)} %all-gather.13.cloned.1.call-done) | copy-start | bytes 9437188
  343.7 6.1 %copy-start.1 = (bf16[2048,768]{1,0:T(8,128)(2,1)S(1)}, bf16[2048,768]{1,0:T(8,128)(2,1)}, u32[]{:S(2)}) copy-start(bf16[2048,768]{1,0:T(8,128)(2,1)} %all-gather.17.cloned.1.call-done) | copy-start | bytes 9437188
Sparse Core Ops, SparseCore 0:
  9.8 31.5 all-gather.10
  43.2 28.6 all-gather.8
  73.8 28.1 all-gather.6
  103.7 28.7 all-gather.12
  134.2 28.7 all-gather.14
  164.6 28.1 all-gather.16
  196.2 70.1 reduce-scatter.1
where the time goes:
time: 364 us; the launch traced here: 359 us
  matrix products  195 us (54%)
  blocking collectives  60.3 us (17%)
  waiting for transfers between devices  40.3 us (11%)
  local copies, waits for them, and re-layouts  26.5 us (7%)
  other arithmetic  22 us (6%)
  between operations  14.4 us (4%)
    psum x1, blocking collectives, device_step(): grad_next = lax.psum(grad_shard.astype(jnp.float32), 'dp')  60.3 us
    dot_general x1, matrix products, local_backward(): jnp.einsum('td,fd->tf', dy_loc, down_full, preferred_element_type=jnp.flo...  42.6 us
    dot_general x1, matrix products, local_backward(): jnp.einsum('td,tf->df', dy_loc, hidden, preferred_element_type=jnp.float32)  28.7 us
    unnamed x12, local copies, waits for them, and re-layouts  26.5 us
    dot_general x1, matrix products, local_backward(): pre_up = jnp.dot(x_loc, up_full, preferred_element_type=jnp.float32)  22.3 us
    dot_general x1, matrix products, local_backward(): pre_gate = jnp.dot(x_loc, gate_full, preferred_element_type=jnp.float32)  22 us
    dot_general x1, matrix products, local_backward(): jnp.einsum('tf,df->td', d_up, up_full, preferred_element_type=jnp.float32)  21.8 us
    all_gather x1, waiting for transfers between devices, device_step(): gate_full = lax.all_gather(w_gate, FSDP_AXES, axis=1, tiled=True)  20.3 us
  transfers between devices with their start and end apart: 7, of which 3 were waited for; matrix products, arithmetic and copies ran while one was open for 66% of the time, Pallas kernels for 0%

commit v1 on v0

v1 whole, which is shorter than its diff:
```python
import functools

import jax
import jax.numpy as jnp
from jax import lax
from jax.experimental import pallas as pl
from jax.experimental.pallas import tpu as pltpu
from jax.sharding import PartitionSpec as P

ALL_AXES = ('dp', 'col', 'fsdp')
FSDP_AXES = ('col', 'fsdp')
MESH = pl.DeviceIdType.MESH
bf16, f32 = jnp.bfloat16, jnp.float32

D, FB, TOK = 768, 256, 4096
T = 1024
NT = TOK // T
NA = 6
HALF = D // 2
VMEM_LIMIT = 67043328


def dot(a, b):
    return jnp.dot(a, b, preferred_element_type=f32)


def dot_nt(a, b):
    return lax.dot_general(a, b, (((1,), (1,)), ((), ())), preferred_element_type=f32)


def dot_tn(a, b):
    return lax.dot_general(a, b, (((0,), (0,)), ((), ())), preferred_element_type=f32)


def rows_of(t):
    return pl.ds(pl.multiple_of(t * T, T), T)


def cols_of(b):
    return pl.ds(pl.multiple_of(b * FB, FB), FB)


def phase1(t, w13, w2, x_v, dy_v, ab_s, dh_s):
    rows = rows_of(t)
    ab_s[...] = dot(x_v[rows, :], w13[...])
    dh_s[...] = dot_nt(dy_v[rows, :], w2[...])


def elementwise(ab_s, dh_s, dab_s, h_s):
    a, b, dh = ab_s[:, :FB], ab_s[:, FB:], dh_s[...]
    s = jax.nn.sigmoid(a)
    act = a * s
    h_s[...] = (act * b).astype(bf16)
    dab_s[:, :FB] = (dh * b * s * (1.0 + a * (1.0 - s))).astype(bf16)
    dab_s[:, FB:] = (dh * act).astype(bf16)


def phase2(t, keep_acc, w13, x_v, dy_v, dab_s, h_s, acc_v, dw13, dw2):
    rows = rows_of(t)
    g13 = dot_tn(x_v[rows, :], dab_s[...])
    dw13[...] = jnp.where(t == 0, 0.0, dw13[...]) + g13
    g2 = dot_tn(dy_v[rows, :], h_s[...])
    dw2[...] = jnp.where(t == 0, 0.0, dw2[...]) + g2
    acc = acc_v[rows, :]
    if keep_acc is not None:
        acc = jnp.where(keep_acc, acc, 0.0)
    acc_v[rows, :] = acc + dot_nt(dab_s[...], w13[...])


class Place:
    def __init__(self):
        self.z = lax.axis_index('dp')
        self.y = lax.axis_index('col')
        f = lax.axis_index('fsdp')
        self.x, self.c = f // 2, f % 2
        x, y, z, c = self.x, self.y, self.z, self.c
        self.dev_c = (z, y, x * 2 + 1 - c)
        self.dev_x = (z, y, (1 - x) * 2 + c)
        self.dev_y = (z, 1 - y, x * 2 + c)
        self.dev_z = (1 - z, y, x * 2 + c)
        self.own = self.block(0, 0, c)

    def block(self, flip_x, flip_y, core):
        x = self.x + flip_x * (1 - 2 * self.x)
        y = self.y + flip_y * (1 - 2 * self.y)
        return (y * 2 + x) * 2 + core

    def order(self, j):
        chip = j // 2
        core = self.c + (j % 2) * (1 - 2 * self.c)
        return self.block(chip % 2, chip // 2, core)


def start(copies):
    for c in copies:
        c.start()


def wait(copies):
    for c in copies:
        c.wait()


def weight_copies(src, w13, w2, sem):
    return (pltpu.make_async_copy(src[0], w13.at[:, pl.ds(0, FB)], sem.at[0]),
            pltpu.make_async_copy(src[1], w13.at[:, pl.ds(FB, FB)], sem.at[1]),
            pltpu.make_async_copy(src[2], w2, sem.at[2]))


def main_kernel(x_h, dy_h, w1_h, w3_h, w2_h, v1_h, v3_h, v2_h, g_h,
                lw1, lw3, lw2, lv1, lv3, lv2, acc_h, dw_h, s_h, rz_h,
                x_v, dy_v, w13_v, w2_v, acc_v, dw13_v, dw2_v, ab_s, dh_s, dab_s, h_s,
                g_st, sp, red, rx, ry, r3,
                xs, ws, os, accs, gl, pps, ppr, axs, axr, bys, byr, r3s, r3r, zs, zr, ssem, ags, agr):
    p = Place()
    n_steps = NA * NT
    own_in = ((w1_h, w3_h, w2_h), (v1_h, v3_h, v2_h))
    land = ((lw1, lw3, lw2), (lv1, lv3, lv2))
    is_s = p.c == p.z
    not_s = p.c != p.z
    blk_c, blk_xc, blk_yc, blk_dc = p.order(1), p.order(2), p.order(4), p.order(6)

    def x_copies(t):
        return (pltpu.make_async_copy(x_h.at[rows_of(t)], x_v.at[rows_of(t)], xs.at[0, t]),
                pltpu.make_async_copy(dy_h.at[rows_of(t)], dy_v.at[rows_of(t)], xs.at[1, t]))

    def w_copies(j, slot):
        if isinstance(j, int) and j == 0:
            src = own_in[0]
        else:
            b = p.order(j)
            src = tuple(a.at[b] for a in land[0])
        return weight_copies(src, w13_v.at[slot], w2_v.at[slot], ws.at[slot])

    def out_copies(j, slot):
        return (pltpu.make_async_copy(dw13_v.at[slot, :, pl.ds(0, FB)], dw_h.at[j, 0], os.at[slot, 0]),
                pltpu.make_async_copy(dw13_v.at[slot, :, pl.ds(FB, FB)], dw_h.at[j, 1], os.at[slot, 1]),
                pltpu.make_async_copy(dw2_v.at[slot], dw_h.at[j, 2], os.at[slot, 2]))

    def acc_copy(t):
        return pltpu.make_async_copy(acc_v.at[rows_of(t)], acc_h.at[rows_of(t)], accs.at[t])

    def ag_copy(k, m, own, b, sid, rid, dev):
        src = own_in[k][m] if own else land[k][m].at[b]
        return pltpu.make_async_remote_copy(
            src_ref=src, dst_ref=land[k][m].at[b], send_sem=ags.at[k, sid, m], recv_sem=agr.at[k, rid, m],
            device_id=dev, device_id_type=MESH)

    routes = ((True, p.own, 0, p.dev_c), (True, p.own, 1, p.dev_x), (False, blk_xc, 4, p.dev_c),
              (False, blk_yc, 5, p.dev_c), (False, blk_dc, 6, p.dev_c), (True, p.own, 2, p.dev_y),
              (False, blk_xc, 3, p.dev_y), (False, blk_yc, 2, p.dev_z), (False, blk_dc, 3, p.dev_z))
    arrivals = (blk_c, blk_xc, blk_yc, blk_dc, p.order(3), p.order(5), p.order(7))

    def send(k, sid, parts=(0, 1, 2)):
        own, b, rid, dev = routes[sid]
        for m in parts:
            ag_copy(k, m, own, b, sid, rid, dev).start()

    def wait_sent(k, sid):
        own, b, rid, dev = routes[sid]
        for m in range(3):
            ag_copy(k, m, own, b, sid, rid, dev).wait_send()

    def arrive(k, rid, parts=(0, 1, 2)):
        for m in parts:
            ag_copy(k, m, False, arrivals[rid], 0, rid, p.dev_c).wait_recv()

    def only(cond, fn):
        pl.when(cond)(fn)

    def own_first(k):
        send(k, 0)
        send(k, 1)

    def got_x(k, parts=(0, 1, 2)):
        arrive(k, 1, parts)
        send(k, 2, parts)
        only(is_s, lambda: send(k, 6, parts))

    def got_y(k):
        arrive(k, 2)
        send(k, 3)
        only(is_s, lambda: send(k, 7))

    def got_d(k):
        arrive(k, 3)
        send(k, 4)
        only(is_s, lambda: send(k, 8))

    def g_load(kind, i, u):
        q, m = i // 3, i % 3
        core = p.c if kind else 1 - p.c
        b = p.block(1 - q // 2, 1 - q % 2, core)
        return pltpu.make_async_copy(g_h.at[0, m, :, cols_of(b)], g_st.at[kind, u], gl.at[kind, u])

    def pair_copy(i):
        return pltpu.make_async_remote_copy(
            src_ref=sp.at[i], dst_ref=red.at[i], send_sem=pps.at[i], recv_sem=ppr.at[i],
            device_id=p.dev_c, device_id_type=MESH)

    LO, HI = pl.ds(0, HALF), pl.ds(HALF, HALF)

    def ax_copy(q, m):
        return pltpu.make_async_remote_copy(
            src_ref=red.at[q * 3 + m, LO], dst_ref=rx.at[q, m], send_sem=axs.at[q, m], recv_sem=axr.at[q, m],
            device_id=p.dev_x, device_id_type=MESH)

    def by_copy(h, m):
        return pltpu.make_async_remote_copy(
            src_ref=red.at[h * 6 + m, HI], dst_ref=ry.at[h, m], send_sem=bys.at[h, m], recv_sem=byr.at[h, m],
            device_id=p.dev_y, device_id_type=MESH)

    def r3_copy(way):
        src = red.at[pl.ds(6, 3), LO] if way == 0 else red.at[pl.ds(3, 3), HI]
        return pltpu.make_async_remote_copy(
            src_ref=src, dst_ref=r3.at[way], send_sem=r3s.at[way], recv_sem=r3r.at[way],
            device_id=p.dev_y if way == 0 else p.dev_x, device_id_type=MESH)

    def z_copy(way):
        rows = LO if way == 0 else HI
        return pltpu.make_async_remote_copy(
            src_ref=red.at[pl.ds(9, 3), rows], dst_ref=rz_h.at[:, rows], send_sem=zs.at[way], recv_sem=zr.at[way],
            device_id=p.dev_z, device_id_type=MESH)

    def s_copy(way):
        rows = LO if way == 0 else HI
        return pltpu.make_async_copy(red.at[pl.ds(9, 3), rows], s_h.at[:, rows], ssem.at[way])

    def add_into(q, rows, got):
        for m in range(3):
            red[q * 3 + m, rows, :] = (red[q * 3 + m, rows, :].astype(f32) + got[m].astype(f32)).astype(bf16)

    def g_part(n):
        @pl.when((n >= 1) & (n <= 6))
        def _():
            for u in range(2):
                pair_copy(2 * (n - 1) + u).start()

        @pl.when((n >= 3) & (n <= 8))
        def _():
            for u in range(2):
                i = 2 * (n - 3) + u
                q, m = i // 3, i % 3

                @pl.when(q < 2)
                def _():
                    ax_copy(q, m).start()

                @pl.when((q == 0) | (q == 2))
                def _():
                    by_copy(q // 2, m).start()

        @pl.when(n <= 5)
        def _():
            for u in range(2):
                i = 2 * n + u
                g_load(0, i, u).wait()
                sp[i] = g_st[0, u].astype(bf16)

                @pl.when(n < 5)
                def _():
                    g_load(0, i + 2, u).start()

        @pl.when((n >= 2) & (n <= 7))
        def _():
            for u in range(2):
                i = 2 * (n - 2) + u
                g_load(1, i, u).wait()
                pair_copy(i).wait_recv()
                red[i] = (red[i].astype(f32) + g_st[1, u].astype(bf16).astype(f32)).astype(bf16)

                @pl.when(n < 7)
                def _():
                    g_load(1, i + 2, u).start()

    def add_rx0():
        for m in range(3):
            ax_copy(0, m).wait_recv()
        add_into(2, LO, rx.at[0])

    def add_ry0():
        for m in range(3):
            by_copy(0, m).wait_recv()
        add_into(1, HI, ry.at[0])

    def add_rx1():
        for m in range(3):
            ax_copy(1, m).wait_recv()
        add_into(3, LO, rx.at[1])

    def add_ry1():
        for m in range(3):
            by_copy(1, m).wait_recv()
        add_into(3, HI, ry.at[1])

    def add_r3(way):
        r3_copy(way).wait_recv()
        add_into(3, LO if way == 0 else HI, r3.at[way])

    def send_z(way):
        z_copy(way).start()
        s_copy(way).start()

    def next_weights(j, rid=None):
        if rid is not None:
            arrive(0, rid)
        start(w_copies(j, j % 2))

    events = {
        2: [lambda: next_weights(1, 0)],
        4: [lambda: only(is_s, lambda: got_y(0))],
        6: [lambda: got_x(0), lambda: next_weights(2)],
        8: [add_ry0],
        9: [lambda: r3_copy(1).start(), lambda: only(not_s, lambda: got_y(0))],
        10: [add_rx0, lambda: next_weights(3, 4), lambda: own_first(1)],
        11: [lambda: r3_copy(0).start(), add_ry1],
        12: [lambda: only(is_s, lambda: send(1, 5))],
        13: [add_rx1, lambda: only(is_s, lambda: got_d(0))],
        14: [lambda: next_weights(4)],
        16: [lambda: add_r3(1), lambda: add_r3(0)],
        17: [lambda: send_z(0), lambda: send_z(1), lambda: only(not_s, lambda: got_d(0))],
        18: [lambda: next_weights(5, 5), lambda: got_x(1, (0,))],
        20: [lambda: got_x(1, (1,)), lambda: only(is_s, lambda: got_y(1))],
        22: [lambda: got_x(1, (2,))],
    }

    start(w_copies(0, 0))
    start(x_copies(0))
    for kind in range(2):
        for u in range(2):
            g_load(kind, u, u).start()
    for t in range(1, NT):
        start(x_copies(t))
    barrier = pltpu.get_barrier_semaphore()
    for dev in (p.dev_c, p.dev_x, p.dev_y, p.dev_z):
        pl.semaphore_signal(barrier, inc=1, device_id=dev, device_id_type=MESH)
    pl.semaphore_wait(barrier, 4)
    own_first(0)
    only(is_s, lambda: send(0, 5))
    wait(w_copies(0, 0))
    wait(x_copies(0))
    phase1(0, w13_v.at[0], w2_v.at[0], x_v, dy_v, ab_s, dh_s)

    def step(n, carry):
        j, t = n // NT, n % NT
        ahead = jnp.minimum(n + 1, n_steps - 1)
        j1, t1 = ahead // NT, ahead % NT
        slot, slot1 = j % 2, j1 % 2

        g_part(n)
        for at, fns in events.items():
            def run(fns=fns):
                for fn in fns:
                    fn()
            pl.when(n == at)(run)

        @pl.when((t == 0) & (j >= 2))
        def _():
            wait(out_copies(j - 2, slot))

        @pl.when((t == NT - 1) & (j + 1 < NA))
        def _():
            wait(w_copies(j + 1, 1 - slot))

        @pl.when(n + 1 < NT)
        def _():
            wait(x_copies(t1))

        elementwise(ab_s, dh_s, dab_s, h_s)
        phase1(t1, w13_v.at[slot1], w2_v.at[slot1], x_v, dy_v, ab_s, dh_s)
        phase2(t, j > 0, w13_v.at[slot], x_v, dy_v, dab_s, h_s, acc_v, dw13_v.at[slot], dw2_v.at[slot])

        @pl.when(t == NT - 1)
        def _():
            start(out_copies(j, slot))

        @pl.when(j == NA - 1)
        def _():
            acc_copy(t).start()

        return carry

    lax.fori_loop(0, n_steps, step, 0)

    only(not_s, lambda: got_y(1))
    got_d(1)
    arrive(0, 6)
    arrive(1, 0)
    for rid in (4, 5, 6):
        arrive(1, rid)
    for way in range(2):
        z_copy(way).wait()
        s_copy(way).wait()
        r3_copy(way).wait_send()
    for i in range(12):
        pair_copy(i).wait_send()
    for q in range(2):
        for m in range(3):
            ax_copy(q, m).wait_send()
            by_copy(q, m).wait_send()
    for k in range(2):
        for sid in range(5):
            wait_sent(k, sid)

    def sent_by_s():
        for k in range(2):
            for sid in range(5, 9):
                wait_sent(k, sid)
    only(is_s, sent_by_s)
    for j in (NA - 2, NA - 1):
        wait(out_copies(j, j % 2))
    for t in range(NT):
        acc_copy(t).wait()


def last_kernel(x_h, dy_h, lw1, lw3, lw2, lv1, lv3, lv2, v1_h, v3_h, v2_h, acc_h, dwa_h, s_h, rz_h,
                dx_h, gn_h, dw_h, o1_h, o3_h, o2_h,
                x_v, dy_v, w13_v, w2_v, acc_v, dw13_v, dw2_v, ab_s, dh_s, dab_s, h_s,
                big, col, row, s_v, rz_v, gn_v,
                xs, ws, os, accs, dxs, ins, outs, sz, gs):
    p = Place()
    nb = 8 - NA
    n_steps = nb * NT

    def x_copies(t):
        return (pltpu.make_async_copy(x_h.at[rows_of(t)], x_v.at[rows_of(t)], xs.at[0, t]),
                pltpu.make_async_copy(dy_h.at[rows_of(t)], dy_v.at[rows_of(t)], xs.at[1, t]))

    def acc_copy(t):
        return pltpu.make_async_copy(acc_h.at[rows_of(t)], acc_v.at[rows_of(t)], accs.at[t])

    def dx_copy(t):
        return pltpu.make_async_copy(dy_v.at[rows_of(t)], dx_h.at[rows_of(t)], dxs.at[t])

    def w_copies(j, slot):
        b = p.order(NA + j)
        return weight_copies(tuple(a.at[b] for a in (lw1, lw3, lw2)), w13_v.at[slot], w2_v.at[slot], ws.at[slot])

    def out_copies(j, slot):
        cols = cols_of(p.order(NA + j))
        return (pltpu.make_async_copy(dw13_v.at[slot, :, pl.ds(0, FB)], dw_h.at[0, :, cols], os.at[slot, 0]),
                pltpu.make_async_copy(dw13_v.at[slot, :, pl.ds(FB, FB)], dw_h.at[1, :, cols], os.at[slot, 1]),
                pltpu.make_async_copy(dw2_v.at[slot], dw_h.at[2, :, cols], os.at[slot, 2]))

    moves = []
    for j in range(NA):
        cols = cols_of(p.order(j))
        for m in range(3):
            moves.append(('big', dwa_h.at[j, m], dw_h.at[m, :, cols]))
    vmoves = []
    for j in range(8):
        b = p.order(j)
        for m, (own, got, out) in enumerate(((v1_h, lv1, o1_h), (v3_h, lv3, o3_h), (v2_h, lv2, o2_h))):
            src = own if j == 0 else got.at[b]
            if m < 2:
                vmoves.append(('col', src, out.at[:, cols_of(b)]))
            else:
                vmoves.append(('row', src, out.at[pl.ds(pl.multiple_of(b * FB, FB), FB)]))
    groups = n_steps - 2
    sets = [moves[g::groups] + vmoves[g::groups] for g in range(groups)]

    def staged(g, way):
        copies, used, half = [], {'big': 0, 'col': 0, 'row': 0}, g % 2
        for k, (kind, src, dst) in enumerate(sets[g]):
            buf = {'big': big, 'col': col, 'row': row}[kind].at[half, used[kind]]
            used[kind] += 1
            if way == 0:
                copies.append(pltpu.make_async_copy(src, buf, ins.at[half, k]))
            else:
                copies.append(pltpu.make_async_copy(buf, dst, outs.at[half, k]))
        return copies

    def sz_copies():
        return (pltpu.make_async_copy(s_h, s_v, sz.at[0]), pltpu.make_async_copy(rz_h, rz_v, sz.at[1]))

    def gn_copy():
        return pltpu.make_async_copy(gn_v, gn_h, gs.at[0])

    start(w_copies(0, 0))
    start(x_copies(0))
    start(x_copies(1))
    acc_copy(0).start()
    for t in range(2, NT):
        start(x_copies(t))
        acc_copy(t - 1).start()
    acc_copy(NT - 1).start()
    for j in range(1, nb):
        start(w_copies(j, j))
    start(sz_copies())
    wait(w_copies(0, 0))
    wait(x_copies(0))
    phase1(0, w13_v.at[0], w2_v.at[0], x_v, dy_v, ab_s, dh_s)

    def dw_next():
        wait(sz_copies())
        for m in range(3):
            gn_v[m] = s_v[m].astype(f32) + rz_v[m].astype(f32)
        gn_copy().start()

    def pass_step(k):
        if 1 <= k <= groups:
            wait(staged(k - 1, 0))
            start(staged(k - 1, 1))
        if k < groups:
            if k >= 2:
                wait(staged(k - 2, 1))
            start(staged(k, 0))

    def step(n, carry):
        j, t = n // NT, n % NT
        ahead = jnp.minimum(n + 1, n_steps - 1)
        j1, t1 = ahead // NT, ahead % NT
        slot, slot1 = j % 2, j1 % 2

        @pl.when(n + 1 < NT)
        def _():
            wait(x_copies(t1))

        @pl.when(n < NT)
        def _():
            acc_copy(t).wait()

        @pl.when((t == NT - 1) & (j + 1 < nb))
        def _():
            wait(w_copies(j + 1, 1 - slot))

        for k in range(n_steps):
            pl.when(n == k)(functools.partial(pass_step, k))
        pl.when(n == 3)(dw_next)

        elementwise(ab_s, dh_s, dab_s, h_s)
        phase1(t1, w13_v.at[slot1], w2_v.at[slot1], x_v, dy_v, ab_s, dh_s)
        phase2(t, None, w13_v.at[slot], x_v, dy_v, dab_s, h_s, acc_v, dw13_v.at[slot], dw2_v.at[slot])

        @pl.when(t == NT - 1)
        def _():
            start(out_copies(j, slot))

        @pl.when(j == nb - 1)
        def _():
            dy_v[rows_of(t), :] = acc_v[rows_of(t), :].astype(bf16)
            dx_copy(t).start()

        return carry

    lax.fori_loop(0, n_steps, step, 0)
    for t in range(NT):
        dx_copy(t).wait()
    for g in (groups - 2, groups - 1):
        wait(staged(g, 1))
    for j in range(nb):
        wait(out_copies(j, j))
    gn_copy().wait()


def compute_scratch():
    return [pltpu.VMEM((TOK, D), bf16), pltpu.VMEM((TOK, D), bf16),
            pltpu.VMEM((2, D, 2 * FB), bf16), pltpu.VMEM((2, FB, D), bf16),
            pltpu.VMEM((TOK, D), f32), pltpu.VMEM((2, D, 2 * FB), f32), pltpu.VMEM((2, D, FB), f32),
            pltpu.VMEM((T, 2 * FB), f32), pltpu.VMEM((T, FB), f32),
            pltpu.VMEM((T, 2 * FB), bf16), pltpu.VMEM((T, FB), bf16)]


def solution(mesh):
    anys = pl.BlockSpec(memory_space=pl.ANY)
    dma = pltpu.SemaphoreType.DMA
    sds = jax.ShapeDtypeStruct

    def device_step(x_loc, dy_loc, w_gate, w_up, w_down, v_gate, v_up, v_down, g_next):
        land = [sds((8, D, FB), bf16), sds((8, D, FB), bf16), sds((8, FB, D), bf16)]
        *gathered, acc, dw_part, g_sum, g_other = pl.pallas_call(
            main_kernel,
            out_shape=land + land + [sds((TOK, D), f32), sds((NA, 3, D, FB), f32),
                                     sds((3, D, FB), bf16), sds((3, D, FB), bf16)],
            in_specs=[anys] * 9, out_specs=[anys] * 10,
            scratch_shapes=compute_scratch() + [
                pltpu.VMEM((2, 2, D, FB), f32), pltpu.VMEM((12, D, FB), bf16), pltpu.VMEM((12, D, FB), bf16),
                pltpu.VMEM((2, 3, HALF, FB), bf16), pltpu.VMEM((2, 3, HALF, FB), bf16),
                pltpu.VMEM((2, 3, HALF, FB), bf16),
                dma((2, NT)), dma((2, 3)), dma((2, 3)), dma((NT,)), dma((2, 2)), dma((12,)), dma((12,)),
                dma((2, 3)), dma((2, 3)), dma((2, 3)), dma((2, 3)), dma((2,)), dma((2,)), dma((2,)), dma((2,)),
                dma((2,)), dma((2, 9, 3)), dma((2, 7, 3))],
            compiler_params=pltpu.CompilerParams(
                collective_id=0, has_side_effects=True, vmem_limit_bytes=VMEM_LIMIT),
            name='main_part',
        )(x_loc, dy_loc, w_gate, w_up, w_down, v_gate, v_up, v_down, g_next)
        dx, grad_next, grad_local, vg, vu, vd = pl.pallas_call(
            last_kernel,
            out_shape=[sds((TOK, D), bf16), sds((3, D, FB), f32), sds((3, D, 8 * FB), f32),
                       sds((D, 8 * FB), bf16), sds((D, 8 * FB), bf16), sds((8 * FB, D), bf16)],
            in_specs=[anys] * 15, out_specs=[anys] * 6,
            scratch_shapes=compute_scratch() + [
                pltpu.VMEM((2, 3, D, FB), f32), pltpu.VMEM((2, 4, D, FB), bf16), pltpu.VMEM((2, 4, FB, D), bf16),
                pltpu.VMEM((3, D, FB), bf16), pltpu.VMEM((3, D, FB), bf16), pltpu.VMEM((3, D, FB), f32),
                dma((2, NT)), dma((2, 3)), dma((2, 3)), dma((NT,)), dma((NT,)), dma((2, 8)), dma((2, 8)),
                dma((2,)), dma((1,))],
            compiler_params=pltpu.CompilerParams(vmem_limit_bytes=VMEM_LIMIT),
            name='last_part',
        )(x_loc, dy_loc, *gathered, v_gate, v_up, v_down, acc, dw_part, g_sum, g_other)
        return dx, grad_next, grad_local[None], vg, vu, vd

    row_spec = P(ALL_AXES, None)
    col_shard = P(None, FSDP_AXES)
    row_shard = P(FSDP_AXES, None)
    dev_spec = P(ALL_AXES, None, None, None)
    return jax.shard_map(
        device_step, mesh=mesh,
        in_specs=(row_spec, row_spec, col_shard, col_shard, row_shard, col_shard, col_shard, row_shard, dev_spec),
        out_specs=(row_spec, P(None, None, FSDP_AXES), dev_spec, P(), P(), P()),
        check_vma=False)
```

time: 364 us -> 183 us (0.50); the launches traced: 359 us -> 183 us
  matrix products: 195 us -> 0 us
  Pallas kernels: 0 us -> 182 us
  blocking collectives: 60.3 us -> 0 us
  waiting for transfers between devices: 40.3 us -> 0 us
  local copies, waits for them, and re-layouts: 26.5 us -> 0 us
  other arithmetic: 22 us -> 0 us
  between operations: 14.4 us -> 0.64 us
    dot_general x8 -> x0, matrix products: 195 us -> none  [the longest x1 42.6 us: local_backward(): jnp.einsum('td,fd->tf', dy_loc, down_full, preferred_element_type=jnp.flo...]
    pallas_call x0 -> x2, Pallas kernels: none -> 182 us  [the longest x1 143 us: device_step(): pl.pallas_call(main_kernel, out_shape=land + land + [sds((TOK, D), f32),...]
    psum x1 -> x0, blocking collectives: 60.3 us -> none  [device_step(): grad_next = lax.psum(grad_shard.astype(jnp.float32), 'dp')]
    all_gather x6 -> x0, waiting for transfers between devices: 36.6 us -> none  [the longest x1 20.3 us: device_step(): gate_full = lax.all_gather(w_gate, FSDP_AXES, axis=1, tiled=True)]
    unnamed x12 -> x0, local copies, waits for them, and re-layouts: 26.5 us -> none
    broadcast_in_dim x1 -> x0, other arithmetic: 12.1 us -> none  [device_step(): grad_local[None]]
    convert_element_type x1 -> x0, other arithmetic: 9.91 us -> none  [device_step(): g_next[0].astype(jnp.bfloat16)]
    unnamed x7 -> x0, waiting for transfers between devices: 3.65 us -> none
  transfers between devices with their start and end apart: 7 -> 0, of which waited for: 3 -> 0; matrix products, arithmetic and copies ran while one was open for 66% -> 0% of each run, Pallas kernels for 0% -> 0%
where the time goes in v1:
time: 183 us
  Pallas kernels  182 us (99%)
    pallas_call x1, Pallas kernels, device_step(): pl.pallas_call(main_kernel, out_shape=land + land + [sds((TOK, D), f32),...  143 us
    pallas_call x1, Pallas kernels, device_step(): pl.pallas_call(last_kernel, out_shape=[sds((TOK, D), bf16), sds((3, D, FB...  39.8 us

profile of v1, /device:TPU:0, one launch (start us, length us, event | category | flops | bytes accessed | tf_op | source)
XLA Modules:
  0.0 183.0 jit_solution(210475866266874601)
XLA Ops:
  0.6 142.5 %main_part.1 = (bf16[8,768,256]{2,1,0:T(8,128)(2,1)}, bf16[8,768,256]{2,1,0:T(8,128)(2,1)}, bf16[8,256,768]{2,1,0:T(8,128)(2,1)}, bf16[8,768,256]{2,1,0:T(8,128)...) custom-call(bf16[4096,768]{1,0:T(8,128)(2,1)} %x_h.3, ...), custom_call_target="tpu_custom_call" | custom-call | tf_op jit(solution)/shard_map/main_part/pallas_call | solution.py:571
  143.2 39.8 %last_part.1 = (bf16[4096,768]{1,0:T(8,128)(2,1)}, f32[3,768,256]{2,1,0:T(8,128)}, f32[3,768,2048]{2,1,0:T(8,128)}, bf16[768,2048]{1,0:T(8,128)(2,1)}, bf16[768,...) custom-call(bf16[4096,768]{1,0:T(8,128)(2,1)} %x_h.3, bf16[4096,768]{1,0:T(8,128)(2,1)} %dy_h.3, ...), custom_call_target="tpu_custom_call" | custom-call | tf_op jit(solution)/shard_map/last_part/pallas_call | solution.py:587

commit v2 on v1

--- a/solution.py
+++ b/solution.py
@@ -15,7 +15,43 @@
 D, FB, TOK = 768, 256, 4096
 T = 1024
 NT = TOK // T
-NA = 6
+NA = 7
+Y_FIRST = False
+PC = 2
+NEXT_AT = 2
+V_AT, V_LAG = (0,1,1), 2
+DW_GROUPS = 3
+SCHEDULE = (
+    ('WoX1', 'WoX0', 'WoC', 'VoX10', 'VoY0', 'VoY2'),
+    ('WoY',),
+    (),
+    ('VoC', 'VoX00'),
+    (),
+    (),
+    ('Wgy1', 'Wgx', 'WgxY'),
+    (),
+    ('VoX11', 'Vgy10'),
+    ('Vgy12',),
+    ('VoY1',),
+    ('Vgx0',),
+    ('Wgy0',),
+    ('Vgy11',),
+    ('ay0', 'VoX01'),
+    ('r3s1', 'Wgd1', 'VgxY0'),
+    ('ax0', 'VoX12'),
+    ('Vgd10', 'Vgx1', 'VgxY1', 'Vgy01'),
+    ('r3s0',),
+    ('Vgd11',),
+    ('ay1', 'ra1', 'VoX02'),
+    ('zs1', 'Vgd01'),
+    ('Vgy00', 'Vgx2', 'VgxY2', 'Vgy02'),
+    ('ax1', 'ra0', 'Vgd12'),
+    ('zs0',),
+    ('Vgd00',),
+    ('Wgd0', 'Vgd02'),
+    (),
+    (),
+)
 HALF = D // 2
 VMEM_LIMIT = 67043328
 
@@ -55,15 +91,19 @@
     dab_s[:, FB:] = (dh * act).astype(bf16)
 
 
+def fresh(t, ref):
+    return ref[...] if isinstance(t, int) else jnp.where(t == 0, 0.0, ref[...])
+
+
 def phase2(t, keep_acc, w13, x_v, dy_v, dab_s, h_s, acc_v, dw13, dw2):
     rows = rows_of(t)
     g13 = dot_tn(x_v[rows, :], dab_s[...])
-    dw13[...] = jnp.where(t == 0, 0.0, dw13[...]) + g13
+    dw13[...] = fresh(t, dw13) + g13
     g2 = dot_tn(dy_v[rows, :], h_s[...])
-    dw2[...] = jnp.where(t == 0, 0.0, dw2[...]) + g2
+    dw2[...] = fresh(t, dw2) + g2
     acc = acc_v[rows, :]
     if keep_acc is not None:
-        acc = jnp.where(keep_acc, acc, 0.0)
+        acc = acc if keep_acc is True else jnp.where(keep_acc, acc, 0.0)
     acc_v[rows, :] = acc + dot_nt(dab_s[...], w13[...])
 
 
@@ -87,8 +127,17 @@
 
     def order(self, j):
         chip = j // 2
-        core = self.c + (j % 2) * (1 - 2 * self.c)
-        return self.block(chip % 2, chip // 2, core)
+        first = self.c + (chip // 3) * (self.z - self.c)
+        core = first + (j % 2) * (1 - 2 * first)
+        return self.block(chip // 2, chip % 2, core) if Y_FIRST else self.block(chip % 2, chip // 2, core)
+
+
+def when(cond, fn):
+    if isinstance(cond, bool):
+        if cond:
+            fn()
+    else:
+        pl.when(cond)(fn)
 
 
 def start(copies):
@@ -116,10 +165,8 @@
     n_steps = NA * NT
     own_in = ((w1_h, w3_h, w2_h), (v1_h, v3_h, v2_h))
     land = ((lw1, lw3, lw2), (lv1, lv3, lv2))
-    is_s = p.c == p.z
-    not_s = p.c != p.z
-    blk_c, blk_xc, blk_yc, blk_dc = p.order(1), p.order(2), p.order(4), p.order(6)
-
+    role = (p.c == p.z, p.c != p.z)
+    blk_c, blk_xc, blk_yc, blk_dc = (p.block(0, 0, 1 - p.c), p.block(1, 0, p.c), p.block(0, 1, p.c), p.block(1, 1, p.c))
     def x_copies(t):
         return (pltpu.make_async_copy(x_h.at[rows_of(t)], x_v.at[rows_of(t)], xs.at[0, t]),
                 pltpu.make_async_copy(dy_h.at[rows_of(t)], dy_v.at[rows_of(t)], xs.at[1, t]))
@@ -149,7 +196,7 @@
     routes = ((True, p.own, 0, p.dev_c), (True, p.own, 1, p.dev_x), (False, blk_xc, 4, p.dev_c),
               (False, blk_yc, 5, p.dev_c), (False, blk_dc, 6, p.dev_c), (True, p.own, 2, p.dev_y),
               (False, blk_xc, 3, p.dev_y), (False, blk_yc, 2, p.dev_z), (False, blk_dc, 3, p.dev_z))
-    arrivals = (blk_c, blk_xc, blk_yc, blk_dc, p.order(3), p.order(5), p.order(7))
+    arrivals = (blk_c, blk_xc, blk_yc, blk_dc, p.block(1, 0, 1 - p.c), p.block(0, 1, 1 - p.c), p.block(1, 1, 1 - p.c))
 
     def send(k, sid, parts=(0, 1, 2)):
         own, b, rid, dev = routes[sid]
@@ -165,27 +212,37 @@
         for m in parts:
             ag_copy(k, m, False, arrivals[rid], 0, rid, p.dev_c).wait_recv()
 
-    def only(cond, fn):
-        pl.when(cond)(fn)
-
-    def own_first(k):
-        send(k, 0)
-        send(k, 1)
-
-    def got_x(k, parts=(0, 1, 2)):
+    def by_role(k, r, fn):
+        pl.when(role[k] if r else role[1 - k])(fn)
+
+    def own_x(k, r, parts):
+        by_role(k, r, lambda: send(k, 1, parts))
+
+    def own_y(k, parts):
+        by_role(k, True, lambda: send(k, 5, parts))
+
+    def got_x(k, parts):
         arrive(k, 1, parts)
         send(k, 2, parts)
-        only(is_s, lambda: send(k, 6, parts))
-
-    def got_y(k):
-        arrive(k, 2)
-        send(k, 3)
-        only(is_s, lambda: send(k, 7))
-
-    def got_d(k):
-        arrive(k, 3)
-        send(k, 4)
-        only(is_s, lambda: send(k, 8))
+
+    def x_to_y(k, parts):
+        by_role(k, True, lambda: send(k, 6, parts))
+
+    def got_y(k, r, parts):
+        def body():
+            arrive(k, 2, parts)
+            send(k, 3, parts)
+            if r:
+                send(k, 7, parts)
+        by_role(k, r, body)
+
+    def got_d(k, r, parts):
+        def body():
+            arrive(k, 3, parts)
+            send(k, 4, parts)
+            if r:
+                send(k, 8, parts)
+        by_role(k, r, body)
 
     def g_load(kind, i, u):
         q, m = i // 3, i % 3
@@ -230,16 +287,17 @@
         for m in range(3):
             red[q * 3 + m, rows, :] = (red[q * 3 + m, rows, :].astype(f32) + got[m].astype(f32)).astype(bf16)
 
+    g_steps = 12 // PC
+
     def g_part(n):
-        @pl.when((n >= 1) & (n <= 6))
-        def _():
-            for u in range(2):
-                pair_copy(2 * (n - 1) + u).start()
-
-        @pl.when((n >= 3) & (n <= 8))
-        def _():
-            for u in range(2):
-                i = 2 * (n - 3) + u
+        def pair_sends():
+            for u in range(PC):
+                pair_copy(PC * (n - 1) + u).start()
+        when((n >= 1) & (n <= g_steps), pair_sends)
+
+        def first_sends():
+            for u in range(PC):
+                i = PC * (n - 3) + u
                 q, m = i // 3, i % 3
 
                 @pl.when(q < 2)
@@ -249,29 +307,30 @@
                 @pl.when((q == 0) | (q == 2))
                 def _():
                     by_copy(q // 2, m).start()
-
-        @pl.when(n <= 5)
-        def _():
-            for u in range(2):
-                i = 2 * n + u
+        when((n >= 3) & (n < 3 + g_steps), first_sends)
+
+        def casts():
+            for u in range(PC):
+                i = PC * n + u
                 g_load(0, i, u).wait()
                 sp[i] = g_st[0, u].astype(bf16)
 
-                @pl.when(n < 5)
+                @pl.when(n < g_steps - 1)
                 def _():
-                    g_load(0, i + 2, u).start()
-
-        @pl.when((n >= 2) & (n <= 7))
-        def _():
-            for u in range(2):
-                i = 2 * (n - 2) + u
+                    g_load(0, i + PC, u).start()
+        when(n < g_steps, casts)
+
+        def pair_adds():
+            for u in range(PC):
+                i = PC * (n - 2) + u
                 g_load(1, i, u).wait()
                 pair_copy(i).wait_recv()
                 red[i] = (red[i].astype(f32) + g_st[1, u].astype(bf16).astype(f32)).astype(bf16)
 
-                @pl.when(n < 7)
+                @pl.when(n < g_steps + 1)
                 def _():
-                    g_load(1, i + 2, u).start()
+                    g_load(1, i + PC, u).start()
+        when((n >= 2) & (n < 2 + g_steps), pair_adds)
 
     def add_rx0():
         for m in range(3):
@@ -301,90 +360,93 @@
         z_copy(way).start()
         s_copy(way).start()
 
-    def next_weights(j, rid=None):
-        if rid is not None:
-            arrive(0, rid)
+    def next_weights(j):
+        if j % 2:
+            arrive(0, {1: 0, 3: 5 if Y_FIRST else 4, 5: 4 if Y_FIRST else 5}[j])
+        if j == 6:
+            by_role(0, False, lambda: arrive(0, 6))
         start(w_copies(j, j % 2))
 
-    events = {
-        2: [lambda: next_weights(1, 0)],
-        4: [lambda: only(is_s, lambda: got_y(0))],
-        6: [lambda: got_x(0), lambda: next_weights(2)],
-        8: [add_ry0],
-        9: [lambda: r3_copy(1).start(), lambda: only(not_s, lambda: got_y(0))],
-        10: [add_rx0, lambda: next_weights(3, 4), lambda: own_first(1)],
-        11: [lambda: r3_copy(0).start(), add_ry1],
-        12: [lambda: only(is_s, lambda: send(1, 5))],
-        13: [add_rx1, lambda: only(is_s, lambda: got_d(0))],
-        14: [lambda: next_weights(4)],
-        16: [lambda: add_r3(1), lambda: add_r3(0)],
-        17: [lambda: send_z(0), lambda: send_z(1), lambda: only(not_s, lambda: got_d(0))],
-        18: [lambda: next_weights(5, 5), lambda: got_x(1, (0,))],
-        20: [lambda: got_x(1, (1,)), lambda: only(is_s, lambda: got_y(1))],
-        22: [lambda: got_x(1, (2,))],
-    }
+    W3 = (0, 1, 2)
+    actions = {
+        'r3s1': lambda: r3_copy(1).start(), 'r3s0': lambda: r3_copy(0).start(),
+        'zs0': lambda: send_z(0), 'zs1': lambda: send_z(1),
+        'WoX1': lambda: own_x(0, True, W3), 'WoX0': lambda: own_x(0, False, W3), 'WoC': lambda: send(0, 0),
+        'WoY': lambda: own_y(0, W3), 'Wgy1': lambda: got_y(0, True, W3), 'Wgx': lambda: got_x(0, W3),
+        'WgxY': lambda: x_to_y(0, W3), 'Wgy0': lambda: got_y(0, False, W3),
+        'Wgd1': lambda: got_d(0, True, W3), 'Wgd0': lambda: got_d(0, False, W3),
+        'ay0': add_ry0, 'ax0': add_rx0, 'ax1': add_rx1, 'ay1': add_ry1,
+        'ra1': lambda: add_r3(1), 'ra0': lambda: add_r3(0), 'VoC': lambda: send(1, 0)}
+    for m in range(3):
+        actions[f'VoX1{m}'] = functools.partial(own_x, 1, True, (m,))
+        actions[f'VoX0{m}'] = functools.partial(own_x, 1, False, (m,))
+        actions[f'VoY{m}'] = functools.partial(own_y, 1, (m,))
+    for m in range(3):
+        actions[f'Vgx{m}'] = functools.partial(got_x, 1, (m,))
+        actions[f'VgxY{m}'] = functools.partial(x_to_y, 1, (m,))
+        actions[f'Vgy1{m}'] = functools.partial(got_y, 1, True, (m,))
+        actions[f'Vgy0{m}'] = functools.partial(got_y, 1, False, (m,))
+        actions[f'Vgd1{m}'] = functools.partial(got_d, 1, True, (m,))
+        actions[f'Vgd0{m}'] = functools.partial(got_d, 1, False, (m,))
+    assert len(SCHEDULE) == n_steps + 1
+    events = {at: [actions[name] for name in names] for at, names in enumerate(SCHEDULE) if names}
+    for j in range(1, NA):
+        events.setdefault(NT * j - 2, []).append(functools.partial(next_weights, j))
+
+    def run_events(at):
+        for fn in events.get(at, []):
+            fn()
 
     start(w_copies(0, 0))
     start(x_copies(0))
-    for kind in range(2):
-        for u in range(2):
-            g_load(kind, u, u).start()
-    for t in range(1, NT):
-        start(x_copies(t))
     barrier = pltpu.get_barrier_semaphore()
     for dev in (p.dev_c, p.dev_x, p.dev_y, p.dev_z):
         pl.semaphore_signal(barrier, inc=1, device_id=dev, device_id_type=MESH)
     pl.semaphore_wait(barrier, 4)
-    own_first(0)
-    only(is_s, lambda: send(0, 5))
+    run_events(0)
     wait(w_copies(0, 0))
     wait(x_copies(0))
+    for kind in range(2):
+        for u in range(PC):
+            g_load(kind, u, u).start()
+    for t in range(1, NT):
+        start(x_copies(t))
     phase1(0, w13_v.at[0], w2_v.at[0], x_v, dy_v, ab_s, dh_s)
 
-    def step(n, carry):
+    def step(n, carry, last=False):
         j, t = n // NT, n % NT
-        ahead = jnp.minimum(n + 1, n_steps - 1)
+        ahead = n if last else n + 1
         j1, t1 = ahead // NT, ahead % NT
         slot, slot1 = j % 2, j1 % 2
 
-        g_part(n)
-        for at, fns in events.items():
-            def run(fns=fns):
-                for fn in fns:
-                    fn()
-            pl.when(n == at)(run)
-
-        @pl.when((t == 0) & (j >= 2))
-        def _():
-            wait(out_copies(j - 2, slot))
-
-        @pl.when((t == NT - 1) & (j + 1 < NA))
-        def _():
-            wait(w_copies(j + 1, 1 - slot))
-
-        @pl.when(n + 1 < NT)
-        def _():
-            wait(x_copies(t1))
+        if last:
+            run_events(n)
+        else:
+            g_part(n)
+            for at in sorted(events):
+                if 0 < at < n_steps - 1:
+                    pl.when(n == at)(functools.partial(run_events, at))
+        when((t == 0) & (j >= 2), lambda: wait(out_copies(j - 2, slot)))
+        if not last:
+            when((t == NT - 1) & (j + 1 < NA), lambda: wait(w_copies(j + 1, 1 - slot)))
+            when(n + 1 < NT, lambda: wait(x_copies(t1)))
 
         elementwise(ab_s, dh_s, dab_s, h_s)
-        phase1(t1, w13_v.at[slot1], w2_v.at[slot1], x_v, dy_v, ab_s, dh_s)
+        if not last:
+            phase1(t1, w13_v.at[slot1], w2_v.at[slot1], x_v, dy_v, ab_s, dh_s)
         phase2(t, j > 0, w13_v.at[slot], x_v, dy_v, dab_s, h_s, acc_v, dw13_v.at[slot], dw2_v.at[slot])
-
-        @pl.when(t == NT - 1)
-        def _():
-            start(out_copies(j, slot))
-
-        @pl.when(j == NA - 1)
-        def _():
-            acc_copy(t).start()
-
+        when(t == NT - 1, lambda: start(out_copies(j, slot)))
+        when(j == NA - 1, lambda: acc_copy(t).start())
         return carry
 
-    lax.fori_loop(0, n_steps, step, 0)
-
-    only(not_s, lambda: got_y(1))
-    got_d(1)
-    arrive(0, 6)
+    lax.fori_loop(0, n_steps - 1, step, 0)
+    step(n_steps - 1, 0, last=True)
+
+    run_events(n_steps)
+    if NA < 7:
+        arrive(0, 6)
+    else:
+        by_role(0, True, lambda: arrive(0, 6))
     arrive(1, 0)
     for rid in (4, 5, 6):
         arrive(1, rid)
@@ -402,11 +464,11 @@
         for sid in range(5):
             wait_sent(k, sid)
 
-    def sent_by_s():
-        for k in range(2):
+    for k in range(2):
+        def relayed(k=k):
             for sid in range(5, 9):
                 wait_sent(k, sid)
-    only(is_s, sent_by_s)
+        pl.when(role[k])(relayed)
     for j in (NA - 2, NA - 1):
         wait(out_copies(j, j % 2))
     for t in range(NT):
@@ -416,8 +478,8 @@
 def last_kernel(x_h, dy_h, lw1, lw3, lw2, lv1, lv3, lv2, v1_h, v3_h, v2_h, acc_h, dwa_h, s_h, rz_h,
                 dx_h, gn_h, dw_h, o1_h, o3_h, o2_h,
                 x_v, dy_v, w13_v, w2_v, acc_v, dw13_v, dw2_v, ab_s, dh_s, dab_s, h_s,
-                big, col, row, s_v, rz_v, gn_v,
-                xs, ws, os, accs, dxs, ins, outs, sz, gs):
+                big, vg_v, vu_v, vd_v, s_v, rz_v, gn_v,
+                xs, ws, os, accs, dxs, ins, outs, vin, vout, sz, gs):
     p = Place()
     nb = 8 - NA
     n_steps = nb * NT
@@ -442,33 +504,29 @@
                 pltpu.make_async_copy(dw13_v.at[slot, :, pl.ds(FB, FB)], dw_h.at[1, :, cols], os.at[slot, 1]),
                 pltpu.make_async_copy(dw2_v.at[slot], dw_h.at[2, :, cols], os.at[slot, 2]))
 
-    moves = []
-    for j in range(NA):
-        cols = cols_of(p.order(j))
-        for m in range(3):
-            moves.append(('big', dwa_h.at[j, m], dw_h.at[m, :, cols]))
-    vmoves = []
-    for j in range(8):
-        b = p.order(j)
-        for m, (own, got, out) in enumerate(((v1_h, lv1, o1_h), (v3_h, lv3, o3_h), (v2_h, lv2, o2_h))):
-            src = own if j == 0 else got.at[b]
-            if m < 2:
-                vmoves.append(('col', src, out.at[:, cols_of(b)]))
+    moves = [(dwa_h.at[j, m], dw_h.at[m, :, cols_of(p.order(j))]) for j in range(NA) for m in range(3)]
+
+    def dw_copies(g, way):
+        half, copies = g % 2, []
+        for k, (src, dst) in enumerate(moves[g::DW_GROUPS]):
+            if way == 0:
+                copies.append(pltpu.make_async_copy(src, big.at[half, k], ins.at[half, k]))
             else:
-                vmoves.append(('row', src, out.at[pl.ds(pl.multiple_of(b * FB, FB), FB)]))
-    groups = n_steps - 2
-    sets = [moves[g::groups] + vmoves[g::groups] for g in range(groups)]
-
-    def staged(g, way):
-        copies, used, half = [], {'big': 0, 'col': 0, 'row': 0}, g % 2
-        for k, (kind, src, dst) in enumerate(sets[g]):
-            buf = {'big': big, 'col': col, 'row': row}[kind].at[half, used[kind]]
-            used[kind] += 1
-            if way == 0:
-                copies.append(pltpu.make_async_copy(src, buf, ins.at[half, k]))
-            else:
-                copies.append(pltpu.make_async_copy(buf, dst, outs.at[half, k]))
+                copies.append(pltpu.make_async_copy(big.at[half, k], dst, outs.at[half, k]))
         return copies
+
+    def v_loads(m):
+        own, got, buf = ((v1_h, lv1, vg_v), (v3_h, lv3, vu_v), (v2_h, lv2, vd_v))[m]
+        copies = []
+        for j in range(8):
+            b = p.order(j)
+            dst = buf.at[pl.ds(pl.multiple_of(b * FB, FB), FB)] if m == 2 else buf.at[:, cols_of(b)]
+            copies.append(pltpu.make_async_copy(own if j == 0 else got.at[b], dst, vin.at[m, j]))
+        return copies
+
+    def v_store(m):
+        src, dst = ((vg_v, o1_h), (vu_v, o3_h), (vd_v, o2_h))[m]
+        return pltpu.make_async_copy(src, dst, vout.at[m])
 
     def sz_copies():
         return (pltpu.make_async_copy(s_h, s_v, sz.at[0]), pltpu.make_async_copy(rz_h, rz_v, sz.at[1]))
@@ -478,17 +536,10 @@
 
     start(w_copies(0, 0))
     start(x_copies(0))
+    wait(w_copies(0, 0))
+    wait(x_copies(0))
     start(x_copies(1))
     acc_copy(0).start()
-    for t in range(2, NT):
-        start(x_copies(t))
-        acc_copy(t - 1).start()
-    acc_copy(NT - 1).start()
-    for j in range(1, nb):
-        start(w_copies(j, j))
-    start(sz_copies())
-    wait(w_copies(0, 0))
-    wait(x_copies(0))
     phase1(0, w13_v.at[0], w2_v.at[0], x_v, dy_v, ab_s, dh_s)
 
     def dw_next():
@@ -498,65 +549,75 @@
         gn_copy().start()
 
     def pass_step(k):
-        if 1 <= k <= groups:
-            wait(staged(k - 1, 0))
-            start(staged(k - 1, 1))
-        if k < groups:
+        if 1 <= k <= DW_GROUPS:
+            wait(dw_copies(k - 1, 0))
+            start(dw_copies(k - 1, 1))
+        if k < DW_GROUPS:
             if k >= 2:
-                wait(staged(k - 2, 1))
-            start(staged(k, 0))
-
-    def step(n, carry):
+                wait(dw_copies(k - 2, 1))
+            start(dw_copies(k, 0))
+        for m in range(3):
+            if k == V_AT[m]:
+                start(v_loads(m))
+            if k == V_AT[m] + V_LAG:
+                wait(v_loads(m))
+                v_store(m).start()
+
+    def step(n, carry, last=False):
         j, t = n // NT, n % NT
-        ahead = jnp.minimum(n + 1, n_steps - 1)
+        ahead = n if last else n + 1
         j1, t1 = ahead // NT, ahead % NT
         slot, slot1 = j % 2, j1 % 2
 
-        @pl.when(n + 1 < NT)
-        def _():
-            wait(x_copies(t1))
-
-        @pl.when(n < NT)
-        def _():
-            acc_copy(t).wait()
-
-        @pl.when((t == NT - 1) & (j + 1 < nb))
-        def _():
-            wait(w_copies(j + 1, 1 - slot))
-
-        for k in range(n_steps):
-            pl.when(n == k)(functools.partial(pass_step, k))
-        pl.when(n == 3)(dw_next)
+        def more_loads():
+            for i in range(1, nb):
+                start(w_copies(i, i))
+            start(sz_copies())
+
+        if last:
+            pass_step(n)
+            when(n < NT, lambda: acc_copy(t).wait())
+        else:
+            when(n + 1 < NT, lambda: wait(x_copies(t1)))
+            when(n + 2 < NT, lambda: start(x_copies(t + 2)))
+            when(n + 1 < NT, lambda: acc_copy(t + 1).start())
+            when(n < NT, lambda: acc_copy(t).wait())
+            when((t == NT - 1) & (j + 1 < nb), lambda: wait(w_copies(j + 1, 1 - slot)))
+            when(n == 1, more_loads)
+            for k in range(n_steps - 1):
+                pl.when(n == k)(functools.partial(pass_step, k))
+            when(n == NEXT_AT, dw_next)
 
         elementwise(ab_s, dh_s, dab_s, h_s)
-        phase1(t1, w13_v.at[slot1], w2_v.at[slot1], x_v, dy_v, ab_s, dh_s)
+        if not last:
+            phase1(t1, w13_v.at[slot1], w2_v.at[slot1], x_v, dy_v, ab_s, dh_s)
         phase2(t, None, w13_v.at[slot], x_v, dy_v, dab_s, h_s, acc_v, dw13_v.at[slot], dw2_v.at[slot])
 
-        @pl.when(t == NT - 1)
-        def _():
-            start(out_copies(j, slot))
-
-        @pl.when(j == nb - 1)
-        def _():
+        when(t == NT - 1, lambda: start(out_copies(j, slot)))
+
+        def finish():
             dy_v[rows_of(t), :] = acc_v[rows_of(t), :].astype(bf16)
             dx_copy(t).start()
-
+        when(j == nb - 1, finish)
         return carry
 
-    lax.fori_loop(0, n_steps, step, 0)
+    lax.fori_loop(0, n_steps - 1, step, 0)
+    step(n_steps - 1, 0, last=True)
     for t in range(NT):
         dx_copy(t).wait()
-    for g in (groups - 2, groups - 1):
-        wait(staged(g, 1))
+    for g in (DW_GROUPS - 2, DW_GROUPS - 1):
+        wait(dw_copies(g, 1))
+    for m in range(3):
+        v_store(m).wait()
     for j in range(nb):
         wait(out_copies(j, j))
     gn_copy().wait()
 
 
-def compute_scratch():
+def compute_scratch(slots):
     return [pltpu.VMEM((TOK, D), bf16), pltpu.VMEM((TOK, D), bf16),
-            pltpu.VMEM((2, D, 2 * FB), bf16), pltpu.VMEM((2, FB, D), bf16),
-            pltpu.VMEM((TOK, D), f32), pltpu.VMEM((2, D, 2 * FB), f32), pltpu.VMEM((2, D, FB), f32),
+            pltpu.VMEM((slots, D, 2 * FB), bf16), pltpu.VMEM((slots, FB, D), bf16),
+            pltpu.VMEM((TOK, D), f32), pltpu.VMEM((slots, D, 2 * FB), f32), pltpu.VMEM((slots, D, FB), f32),
             pltpu.VMEM((T, 2 * FB), f32), pltpu.VMEM((T, FB), f32),
             pltpu.VMEM((T, 2 * FB), bf16), pltpu.VMEM((T, FB), bf16)]
 
@@ -573,26 +634,28 @@
             out_shape=land + land + [sds((TOK, D), f32), sds((NA, 3, D, FB), f32),
                                      sds((3, D, FB), bf16), sds((3, D, FB), bf16)],
             in_specs=[anys] * 9, out_specs=[anys] * 10,
-            scratch_shapes=compute_scratch() + [
-                pltpu.VMEM((2, 2, D, FB), f32), pltpu.VMEM((12, D, FB), bf16), pltpu.VMEM((12, D, FB), bf16),
+            scratch_shapes=compute_scratch(2) + [
+                pltpu.VMEM((2, PC, D, FB), f32), pltpu.VMEM((12, D, FB), bf16), pltpu.VMEM((12, D, FB), bf16),
                 pltpu.VMEM((2, 3, HALF, FB), bf16), pltpu.VMEM((2, 3, HALF, FB), bf16),
                 pltpu.VMEM((2, 3, HALF, FB), bf16),
-                dma((2, NT)), dma((2, 3)), dma((2, 3)), dma((NT,)), dma((2, 2)), dma((12,)), dma((12,)),
+                dma((2, NT)), dma((2, 3)), dma((2, 3)), dma((NT,)), dma((2, PC)), dma((12,)), dma((12,)),
                 dma((2, 3)), dma((2, 3)), dma((2, 3)), dma((2, 3)), dma((2,)), dma((2,)), dma((2,)), dma((2,)),
                 dma((2,)), dma((2, 9, 3)), dma((2, 7, 3))],
             compiler_params=pltpu.CompilerParams(
                 collective_id=0, has_side_effects=True, vmem_limit_bytes=VMEM_LIMIT),
             name='main_part',
         )(x_loc, dy_loc, w_gate, w_up, w_down, v_gate, v_up, v_down, g_next)
+        n_big = -(-3 * NA // DW_GROUPS)
         dx, grad_next, grad_local, vg, vu, vd = pl.pallas_call(
             last_kernel,
             out_shape=[sds((TOK, D), bf16), sds((3, D, FB), f32), sds((3, D, 8 * FB), f32),
                        sds((D, 8 * FB), bf16), sds((D, 8 * FB), bf16), sds((8 * FB, D), bf16)],
             in_specs=[anys] * 15, out_specs=[anys] * 6,
-            scratch_shapes=compute_scratch() + [
-                pltpu.VMEM((2, 3, D, FB), f32), pltpu.VMEM((2, 4, D, FB), bf16), pltpu.VMEM((2, 4, FB, D), bf16),
+            scratch_shapes=compute_scratch(min(2, 8 - NA)) + [
+                pltpu.VMEM((2, n_big, D, FB), f32),
+                pltpu.VMEM((D, 8 * FB), bf16), pltpu.VMEM((D, 8 * FB), bf16), pltpu.VMEM((8 * FB, D), bf16),
                 pltpu.VMEM((3, D, FB), bf16), pltpu.VMEM((3, D, FB), bf16), pltpu.VMEM((3, D, FB), f32),
-                dma((2, NT)), dma((2, 3)), dma((2, 3)), dma((NT,)), dma((NT,)), dma((2, 8)), dma((2, 8)),
+                dma((2, NT)), dma((2, 3)), dma((2, 3)), dma((NT,)), dma((NT,)), dma((2, n_big)), dma((2, n_big)), dma((3, 8)), dma((3,)),
                 dma((2,)), dma((1,))],
             compiler_params=pltpu.CompilerParams(vmem_limit_bytes=VMEM_LIMIT),
             name='last_part',

time: 183 us -> 157 us (0.86)
  Pallas kernels: 182 us -> 156 us
    pallas_call x1, Pallas kernels: 143 us -> 125 us  [device_step(): pl.pallas_call(main_kernel, out_shape=land + land + [sds((TOK, D), f32),...]
    pallas_call x1, Pallas kernels: 39.8 us -> 31.5 us  [device_step(): pl.pallas_call(last_kernel, out_shape=[sds((TOK, D), bf16), sds((3, D, FB...]
where the time goes in v2:
time: 157 us
  Pallas kernels  156 us (99%)
    pallas_call x1, Pallas kernels, device_step(): pl.pallas_call(main_kernel, out_shape=land + land + [sds((TOK, D), f32),...  125 us
    pallas_call x1, Pallas kernels, device_step(): pl.pallas_call(last_kernel, out_shape=[sds((TOK, D), bf16), sds((3, D, FB...  31.5 us

profile of v2, /device:TPU:0, one launch (start us, length us, event | category | flops | bytes accessed | tf_op | source)
XLA Modules:
  0.0 157.2 jit_solution(9700545222544891479)
XLA Ops:
  0.6 124.9 %main_part.1 = (bf16[8,768,256]{2,1,0:T(8,128)(2,1)}, bf16[8,768,256]{2,1,0:T(8,128)(2,1)}, bf16[8,256,768]{2,1,0:T(8,128)(2,1)}, bf16[8,768,256]{2,1,0:T(8,128)...) custom-call(bf16[4096,768]{1,0:T(8,128)(2,1)} %x_h.3, ...), custom_call_target="tpu_custom_call" | custom-call | tf_op jit(solution)/shard_map/main_part/pallas_call | solution.py:632
  125.5 31.5 %last_part.1 = (bf16[4096,768]{1,0:T(8,128)(2,1)}, f32[3,768,256]{2,1,0:T(8,128)}, f32[3,768,2048]{2,1,0:T(8,128)}, bf16[768,2048]{1,0:T(8,128)(2,1)}, bf16[768,...) custom-call(bf16[4096,768]{1,0:T(8,128)(2,1)} %x_h.3, bf16[4096,768]{1,0:T(8,128)(2,1)} %dy_h.3, ...), custom_call_target="tpu_custom_call" | custom-call | tf_op jit(solution)/shard_map/last_part/pallas_call | solution.py:649
